TPU v7x, 16 devices: a 4x2x1 block of a 4x4x8 slice. The times are simulated.
16 devices in a mesh: rep: 2 (over y, z), dp: 8 (over x, core).
Axes of the slice: x: 4, y: 2, z: 1, core: 2. Of those that a mesh axis runs over, the one named last changes fastest.
The devices are a block of a 4x4x8 slice.
Arguments:
- a: bfloat16 [16, 4, 4096, 896], P(('rep', 'dp')), parts along dimension 0
- g: bfloat16 [16, 4, 4096, 2560], P(('rep', 'dp')), parts along dimension 0
Outputs:
- output: bfloat16 [8, 896, 2560], P('rep'), parts along dimension 0
There are 2 independent parts. A program takes and returns all parts, laid end to end along the dimension named above; each array names one.
All inputs are finite; a program needn't handle non-finite values.
Results may differ from a plain program's by a relative error of at most 0.012.
Values are sent between devices in bfloat16 or wider.
A program may use at most 768 MiB of HBM per device.

v0:
```python
import jax
import jax.numpy as jnp


def solution(mesh):
    groups = mesh.shape["rep"]

    def step(a, g):
        a, g = (t.reshape(groups, -1, *t.shape[1:]) for t in (a, g))
        sums = jnp.einsum("rsntd,rsntf->rndf", a, g, preferred_element_type=jnp.float32)
        return sums.astype(jnp.bfloat16).reshape(-1, *sums.shape[2:])

    return step
```

profile of v0, /device:TPU:113, one launch (start us, length us, event | category | flops | bytes accessed | tf_op | source)
XLA Modules:
  0.0 456.1 jit_solution(5421307104811361520)
XLA Ops:
  0.0 87.3 %fusion.3 = f32[1,4,896,2560]{3,2,1,0:T(8,128)} fusion(bf16[1,4,4096,2560]{3,2,1,0:T(8,128)(2,1)} %param.1, bf16[1,4,4096,896]{3,2,1,0:T(8,128)(2,1)} %param), kind=kOutput, calls=%fused_computation.3 | convolution fusion | flops 75161927680 | bytes 149946368 | tf_op jit(solution)/rsntd,rsntf->rndf/dot_general | solution.py:10
  87.3 368.7 %all-reduce.2 = bf16[1,4,896,2560]{3,2,1,0:T(8,128)(2,1)} all-reduce(f32[1,4,896,2560]{3,2,1,0:T(8,128)} %fusion.3), channel_id=1, replica_groups=[2,8]<=[16], use_global_device_ids=true, to_apply=%add.clone | all-reduce | flops 9175040 | bytes 55050240 | tf_op jit(solution)/rsntd,rsntf->rndf/dot_general | solution.py:10
where the time goes:
time: 458 us; the launch traced here: 456 us
  blocking collectives  369 us (81%)
  matrix products  87.3 us (19%)
    dot_general x1, blocking collectives, step(): jnp.einsum('rsntd,rsntf->rndf', a, g, preferred_element_type=jnp.float32)  369 us
    dot_general x1, matrix products, step(): jnp.einsum('rsntd,rsntf->rndf', a, g, preferred_element_type=jnp.float32)  87.3 us

commit v1 on v0

v1 whole, which is shorter than its diff:
```python
import functools

import jax
import jax.numpy as jnp
from jax import lax
from jax.experimental import pallas as pl
from jax.experimental.pallas import tpu as pltpu
from jax.sharding import PartitionSpec as P

MESH = pl.DeviceIdType.MESH
CORES = 2
COLS = 256
BLOCKS = 2
SLOTS = 10
ACCS = 4
G_SLOTS = 3
LAG_A, LAG_B, LAG_C = 1, 2, 3
LAG_E, LAG_F, LAG_G = 3, 6, 8


def when(cond):
    return pl.when(cond)


def kernel(chips, mats, chunks_per, cols, blocks, a_hbm, g_hbm, out, a_buf, g_buf, acc, sib_out, sib_in, far_out, far_in,
           dir_out, dir_in, sum_out, sum_in, a_sem, g_sem, rs_send, rs_recv, ag_send, ag_recv, pair_send, pair_recv):
    me = lax.axis_index("dp")
    x, c = me // CORES, me % CORES
    chunks = mats * chunks_per
    tokens = a_hbm.shape[1]
    step = tokens // blocks
    partner = {"dp": x * CORES + (1 - c)}

    def chip(delta):
        return lax.rem(x + delta + chips, chips)

    def at(d):
        return {"dp": d * CORES + c}

    def ways(k):
        s = 1 - 2 * lax.rem(k, 2)
        return chip(s), chip(-s)

    far = chip(2)

    def a_copy(n, b):
        rows = pl.ds(b * step, step)
        return pltpu.make_async_copy(a_hbm.at[n, rows], a_buf.at[lax.rem(n, 2), rows], a_sem.at[lax.rem(n, 2), b])

    def g_copy(k, b):
        rows = pl.ds(b * step, step)
        slot = lax.rem(k, G_SLOTS)
        columns = pl.ds(pl.multiple_of(lax.rem(k, chunks_per) * cols, cols), cols)
        return pltpu.make_async_copy(g_hbm.at[k // chunks_per, rows, columns], g_buf.at[slot, rows], g_sem.at[slot, b])

    def remote(src, dst, send, recv, to):
        return pltpu.make_async_remote_copy(src_ref=src, dst_ref=dst, send_sem=send, recv_sem=recv, device_id=to,
                                            device_id_type=MESH)

    def rs(k, kind, src, dst, to):
        slot = lax.rem(k, SLOTS)
        return remote(src.at[slot], dst.at[slot], rs_send.at[kind, slot], rs_recv.at[kind, slot], to)

    def swap(k):
        return rs(k, 0, sib_out, sib_in, partner)

    def hop_far(k):
        return rs(k, 1, far_out, far_in, at(ways(k)[1]))

    def hop_direct(k):
        return rs(k, 2, dir_out, dir_in, at(ways(k)[0]))

    def hop_sum(k):
        return rs(k, 3, sum_out, sum_in, at(ways(k)[1]))

    def place(k, d):
        columns = pl.ds(pl.multiple_of(lax.rem(k, chunks_per) * cols, cols), cols)
        return out.at[k // chunks_per, d, c, :, columns]

    def gather(k, kind, d, to):
        return remote(place(k, d), place(k, d), ag_send.at[kind, k], ag_recv.at[kind, k], at(to))

    def pair(k):
        columns = pl.ds(pl.multiple_of(lax.rem(k, chunks_per) * cols, cols), cols)
        block = out.at[k // chunks_per, :, c, :, columns]
        return remote(block, block, pair_send.at[k], pair_recv.at[k], partner)

    for b in range(blocks):
        a_copy(0, b).start()
        g_copy(0, b).start()
    for b in range(blocks):
        g_copy(1, b).start()
    barrier = pltpu.get_barrier_semaphore()
    for to in (partner, at(chip(1)), at(chip(-1))):
        pl.semaphore_signal(barrier, inc=1, device_id=to, device_id_type=MESH)
    pl.semaphore_wait(barrier, 3)

    def stage_matmul(k):
        @when(k + 2 < chunks)
        def _():
            for b in range(blocks):
                g_copy(k + 2, b).start()

        n, first = k // chunks_per, lax.rem(k, chunks_per) == 0

        @when(first & (n + 1 < mats))
        def _():
            for b in range(blocks):
                a_copy(n + 1, b).start()

        slot, g_slot, a_slot = lax.rem(k, ACCS), lax.rem(k, G_SLOTS), lax.rem(n, 2)
        for b in range(blocks):
            @when(first)
            def _():
                a_copy(n, b).wait()

            g_copy(k, b).wait()
            rows = pl.ds(b * step, step)
            part = lax.dot_general(a_buf[a_slot, rows], g_buf[g_slot, rows], (((0,), (0,)), ((), ())),
                                   preferred_element_type=jnp.float32)
            part = part.reshape(acc.shape[1:])
            if b == 0:
                acc[slot] = part
            else:
                acc[slot] += part

        @when(k >= SLOTS)
        def _():
            swap(k - SLOTS).wait_send()

        rs_slot = lax.rem(k, SLOTS)
        for d in range(chips):
            sib_out[rs_slot, d] = acc[slot, d * CORES + 1 - c].astype(jnp.bfloat16)
        swap(k).start()

    def mine(k, d):
        return acc[lax.rem(k, ACCS), d * CORES + c] + sib_in[lax.rem(k, SLOTS), d].astype(jnp.float32)

    def stage_a(k):
        slot = lax.rem(k, SLOTS)
        swap(k).wait_recv()

        @when(k >= SLOTS)
        def _():
            hop_far(k - SLOTS).wait_send()
            hop_direct(k - SLOTS).wait_send()

        far_out[slot] = mine(k, far).astype(jnp.bfloat16)
        hop_far(k).start()
        dir_out[slot] = mine(k, ways(k)[0]).astype(jnp.bfloat16)
        hop_direct(k).start()

    def stage_b(k):
        slot = lax.rem(k, SLOTS)
        hop_far(k).wait_recv()

        @when(k >= SLOTS)
        def _():
            hop_sum(k - SLOTS).wait_send()

        sum_out[slot] = (mine(k, ways(k)[1]) + far_in[slot].astype(jnp.float32)).astype(jnp.bfloat16)
        hop_sum(k).start()

    def stage_c(k):
        slot = lax.rem(k, SLOTS)
        hop_direct(k).wait_recv()
        hop_sum(k).wait_recv()
        total = mine(k, x) + dir_in[slot].astype(jnp.float32) + sum_in[slot].astype(jnp.float32)
        place(k, x)[...] = total.astype(jnp.bfloat16)

    def stage_d(k):
        forth, back = ways(k)
        gather(k, 0, x, forth).start()
        gather(k, 1, x, back).start()

    def stage_e(k):
        forth, back = ways(k)
        gather(k, 0, back, forth).wait_recv()
        gather(k, 2, back, forth).start()
        gather(k, 1, forth, back).wait_recv()

    def stage_f(k):
        forth, back = ways(k)
        gather(k, 2, far, forth).wait_recv()
        pair(k).start()

    def stage_g(k):
        forth, back = ways(k)
        gather(k, 0, x, forth).wait_send()
        gather(k, 1, x, back).wait_send()
        gather(k, 2, back, forth).wait_send()
        pair(k).wait_recv()
        pair(k).wait_send()

    def spread(t):
        return (t // 3) * 2 + lax.rem(t, 3), lax.rem(t, 3) < 2

    def tick(t, _):
        for stage, lag in ((stage_a, LAG_A), (stage_b, LAG_B), (stage_c, LAG_C)):
            k = t - lag

            @when((k >= 0) & (k < chunks))
            def _():
                stage(k)

        for stage, lag in ((stage_d, 0), (stage_e, LAG_E), (stage_f, LAG_F), (stage_g, LAG_G)):
            u = t - lag - LAG_C
            k, there = spread(jnp.maximum(u, 0))

            @when((u >= 0) & there & (k < chunks))
            def _():
                stage(k)

        @when(t < chunks)
        def _():
            stage_matmul(t)

        return 0

    last = ((chunks - 1) // 2) * 3 + (chunks - 1) % 2
    lax.fori_loop(0, LAG_C + last + LAG_G + 1, tick, 0)

    def drain(i, _):
        k = chunks - SLOTS + i
        swap(k).wait_send()
        hop_far(k).wait_send()
        hop_direct(k).wait_send()
        hop_sum(k).wait_send()
        return 0

    lax.fori_loop(0, SLOTS, drain, 0)


def solution(mesh):
    group = mesh.shape["dp"]
    chips = group // CORES

    def local(a, g):
        _, mats, tokens, rows = a.shape
        width = g.shape[-1]
        piece = rows // group
        chunks_per = width // COLS
        chunks = mats * chunks_per
        shape = (mats, chips, CORES, piece, width)
        bf16, f32 = jnp.bfloat16, jnp.float32
        many, one = (SLOTS, chips, piece, COLS), (SLOTS, piece, COLS)
        dma = pltpu.SemaphoreType.DMA
        flops = 2 * mats * tokens * rows * width
        sums = pl.pallas_call(
            functools.partial(kernel, chips, mats, chunks_per, COLS, BLOCKS),
            out_shape=pltpu.VMEM(shape, bf16),
            in_specs=[pl.BlockSpec(memory_space=pl.ANY)] * 2,
            out_specs=pl.BlockSpec(memory_space=pltpu.VMEM),
            scratch_shapes=[
                pltpu.VMEM((2, tokens, rows), bf16),
                pltpu.VMEM((G_SLOTS, tokens, COLS), bf16),
                pltpu.VMEM((ACCS, group, piece, COLS), f32),
                pltpu.VMEM(many, bf16), pltpu.VMEM(many, bf16),
                pltpu.VMEM(one, bf16), pltpu.VMEM(one, bf16),
                pltpu.VMEM(one, bf16), pltpu.VMEM(one, bf16),
                pltpu.VMEM(one, bf16), pltpu.VMEM(one, bf16),
                dma((2, BLOCKS)), dma((G_SLOTS, BLOCKS)),
                dma((4, SLOTS)), dma((4, SLOTS)),
                dma((3, chunks)), dma((3, chunks)),
                dma((chunks,)), dma((chunks,)),
            ],
            compiler_params=pltpu.CompilerParams(collective_id=0, has_side_effects=True, vmem_limit_bytes=VMEM_LIMIT),
            cost_estimate=pl.CostEstimate(flops=flops, bytes_accessed=a.nbytes + g.nbytes, transcendentals=0),
            name="grad_sums",
        )(a.reshape(a.shape[1:]), g.reshape(g.shape[1:]))
        return sums.reshape(mats, rows, width)

    return jax.shard_map(local, mesh=mesh, in_specs=(P(("rep", "dp")),) * 2, out_specs=P("rep"), check_vma=False)


VMEM_LIMIT = 44 * 2**20
```

time: 458 us -> 282 us (0.62)
  blocking collectives: 369 us -> 0 us
  Pallas kernels: 0 us -> 276 us
  matrix products: 87.3 us -> 0 us
  local copies, waits for them, and re-layouts: 0 us -> 6.68 us
    dot_general x1 -> x0, blocking collectives: 369 us -> none  [step(): jnp.einsum('rsntd,rsntf->rndf', a, g, preferred_element_type=jnp.float32)]
    pallas_call x0 -> x1, Pallas kernels: none -> 276 us  [local(): pl.pallas_call(functools.partial(kernel, chips, mats, chunks_per, COLS, B...]
    dot_general x1 -> x0, matrix products: 87.3 us -> none  [step(): jnp.einsum('rsntd,rsntf->rndf', a, g, preferred_element_type=jnp.float32)]
    unnamed x0 -> x1, local copies, waits for them, and re-layouts: none -> 6.68 us
where the time goes in v1:
time: 282 us
  Pallas kernels  276 us (98%)
  local copies, waits for them, and re-layouts  6.68 us (2%)
    pallas_call x1, Pallas kernels, local(): pl.pallas_call(functools.partial(kernel, chips, mats, chunks_per, COLS, B...  276 us
    unnamed x1, local copies, waits for them, and re-layouts  6.68 us

profile of v1, /device:TPU:113, one launch (start us, length us, event | category | flops | bytes accessed | tf_op | source)
XLA Modules:
  0.0 282.4 jit_solution(14821215338541735940)
XLA Ops:
  0.0 275.7 %grad_sums.1 = bf16[4,4,2,112,2560]{4,3,2,1,0:T(8,128)(2,1)S(1)} custom-call(bf16[4,4096,896]{2,1,0:T(8,128)(2,1)} %bitcast.4, bf16[4,4096,2560]{2,1,0:T(8,128)(2,1)} %bitcast.1.g_hbm), custom_call_target="tpu_custom_call" | custom-call | flops 75161927680 | bytes 113246208 | tf_op jit(solution)/shard_map/grad_sums/pallas_call | solution.py:249
  275.7 6.7 %copy.4 = bf16[4,896,2560]{2,1,0:T(8,128)(2,1)} copy(bf16[4,896,2560]{2,1,0:T(8,128)(2,1)S(1)} %bitcast.3) | data formatting | bytes 36700160

commit v2 on v1

--- a/solution.py
+++ b/solution.py
@@ -10,12 +10,12 @@
 MESH = pl.DeviceIdType.MESH
 CORES = 2
 COLS = 256
-BLOCKS = 2
-SLOTS = 10
-ACCS = 4
+BLOCKS = 1
+SLOTS = 12
+ACCS = 7
 G_SLOTS = 3
-LAG_A, LAG_B, LAG_C = 1, 2, 3
-LAG_E, LAG_F, LAG_G = 3, 6, 8
+LAG_A, LAG_B, LAG_C = 2, 4, 6
+LAG_E, LAG_F, LAG_G = 5, 10, 13
 
 
 def when(cond):

time: 282 us -> 177 us (0.63)
  Pallas kernels: 276 us -> 170 us
    pallas_call x1, Pallas kernels: 276 us -> 170 us  [local(): pl.pallas_call(functools.partial(kernel, chips, mats, chunks_per, COLS, B...]
where the time goes in v2:
time: 177 us
  Pallas kernels  170 us (96%)
  local copies, waits for them, and re-layouts  6.68 us (4%)
    pallas_call x1, Pallas kernels, local(): pl.pallas_call(functools.partial(kernel, chips, mats, chunks_per, COLS, B...  170 us
    unnamed x1, local copies, waits for them, and re-layouts  6.68 us

profile of v2, /device:TPU:113, one launch (start us, length us, event | category | flops | bytes accessed | tf_op | source)
XLA Modules:
  0.0 177.0 jit_solution(1427375068720711759)
XLA Ops:
  0.0 170.3 %grad_sums.1 = bf16[4,4,2,112,2560]{4,3,2,1,0:T(8,128)(2,1)S(1)} custom-call(bf16[4,4096,896]{2,1,0:T(8,128)(2,1)} %bitcast.4, bf16[4,4096,2560]{2,1,0:T(8,128)(2,1)} %bitcast.1.g_hbm), custom_call_target="tpu_custom_call" | custom-call | flops 75161927680 | bytes 113246208 | tf_op jit(solution)/shard_map/grad_sums/pallas_call | solution.py:249
  170.3 6.7 %copy.4 = bf16[4,896,2560]{2,1,0:T(8,128)(2,1)} copy(bf16[4,896,2560]{2,1,0:T(8,128)(2,1)S(1)} %bitcast.3) | data formatting | bytes 36700160

commit v3 on v2

v3 whole, which is shorter than its diff:
```python
import functools

import jax
import jax.numpy as jnp
from jax import lax
from jax.experimental import pallas as pl
from jax.experimental.pallas import tpu as pltpu
from jax.sharding import PartitionSpec as P

MESH = pl.DeviceIdType.MESH
CORES = 2
COLS = 256
SLOTS = 12
ACCS = 7
G_SLOTS = 3
AG_SLOTS = 12
EARLY = 0
LAG_A, LAG_B, LAG_C = (1, 1), (3, 3), (5, 5)
LAG_D1, LAG_E, LAG_F, LAG_G = 0, 4, 7, 9


def when(cond):
    return pl.when(cond)


def kernel(chips, mats, chunks_per, cols, a_hbm, g_hbm, out, a_buf, g_buf, acc, sib_out, sib_in, far_out, far_in,
           dir_out, dir_in, sum_out, sum_in, a_sem, first_sem, g_sem, rs_send, rs_recv, ag_send, ag_recv, pair_send, pair_recv):
    me = lax.axis_index("dp")
    x, c = me // CORES, me % CORES
    chunks = mats * chunks_per
    tokens = a_hbm.shape[1]
    rows = a_hbm.shape[2]
    piece = rows // (chips * CORES)
    cuts = [0, rows]
    split = -(-rows // 256) * 128
    partner = {"dp": x * CORES + (1 - c)}

    def chip(delta):
        return lax.rem(x + delta + chips, chips)

    def at(d):
        return {"dp": d * CORES + c}

    def ways(k):
        s = 1 - 2 * lax.rem(k, 2)
        return chip(s), chip(-s)

    far = chip(2)

    def a_copy(n):
        return pltpu.make_async_copy(a_hbm.at[n], a_buf.at[lax.rem(n, 2)], a_sem.at[lax.rem(n, 2)])

    def first_copy(i):
        part = pl.ds(cuts[i], cuts[i + 1] - cuts[i])
        return pltpu.make_async_copy(a_hbm.at[0, :, part], a_buf.at[0, :, part], first_sem.at[i])

    def g_copy(k):
        slot = lax.rem(k, G_SLOTS)
        return pltpu.make_async_copy(g_hbm.at[k // chunks_per, :, columns_of(k)], g_buf.at[slot], g_sem.at[slot])

    def columns_of(k):
        return pl.ds(pl.multiple_of(lax.rem(k, chunks_per) * cols, cols), cols)

    def remote(src, dst, send, recv, to):
        return pltpu.make_async_remote_copy(src_ref=src, dst_ref=dst, send_sem=send, recv_sem=recv, device_id=to,
                                            device_id_type=MESH)

    def rs(k, kind, src, dst, to):
        slot = lax.rem(k, SLOTS)
        return remote(src.at[slot], dst.at[slot], rs_send.at[min(kind, 1), slot], rs_recv.at[kind, slot], to)

    def swap(k):
        return rs(k, 0, sib_out, sib_in, partner)

    def hops_left(k):
        slot = lax.rem(k, SLOTS)
        three = sib_out.at[slot, pl.ds(0, 3)]
        remote(three, three, rs_send.at[1, slot], rs_recv.at[0, slot], partner).wait_send()

    def hop_far(k):
        return rs(k, 1, far_out, far_in, at(ways(k)[1]))

    def hop_direct(k):
        return rs(k, 2, dir_out, dir_in, at(ways(k)[0]))

    def hop_sum(k):
        return rs(k, 3, sum_out, sum_in, at(ways(k)[1]))

    def place(k, d):
        return out.at[k // chunks_per, d, c, :, columns_of(k)]

    def gather(k, kind, d, to):
        slot = lax.rem(k, AG_SLOTS)
        return remote(place(k, d), place(k, d), ag_send.at[slot], ag_recv.at[kind, slot], at(to))

    def pair(k):
        block = out.at[k // chunks_per, :, c, :, columns_of(k)]
        slot = lax.rem(k, AG_SLOTS)
        return remote(block, block, pair_send.at[slot], pair_recv.at[slot], partner)

    g_copy(0).start()
    for i in range(len(cuts) - 1):
        first_copy(i).start()
    barrier = pltpu.get_barrier_semaphore()
    for to in (partner, at(chip(1)), at(chip(-1))):
        pl.semaphore_signal(barrier, inc=1, device_id=to, device_id_type=MESH)

    def send_half(k):
        @when(k >= SLOTS)
        def _():
            swap(k - SLOTS).wait_send()

        for d in range(chips):
            sib_out[lax.rem(k, SLOTS), d] = terms(k, d, 1 - c).astype(jnp.bfloat16)
        swap(k).start()

    def terms(k, d, core):
        return acc[lax.rem(k, ACCS), pl.ds(pl.multiple_of((d * CORES + core) * piece, piece), piece)]

    def multiply(k, tokens_of, rows_of):
        return lax.dot_general(a_buf[lax.rem(k // chunks_per, 2), tokens_of, rows_of], g_buf[lax.rem(k, G_SLOTS), tokens_of],
                               (((0,), (0,)), ((), ())), preferred_element_type=jnp.float32)

    def start_loads(k):
        @when(k < chunks)
        def _():
            g_copy(k).start()

    def ready(k):
        n, first = k // chunks_per, lax.rem(k, chunks_per) == 0

        @when(first & (n + 1 < mats))
        def _():
            a_copy(n + 1).start()

        @when(first)
        def _():
            a_copy(n).wait()

        g_copy(k).wait()

    def part_matmul(k, lo, hi):
        acc[lax.rem(k, ACCS), pl.ds(lo, hi - lo)] = multiply(k, pl.ds(0, tokens), pl.ds(lo, hi - lo))

    def mine(k, d):
        return terms(k, d, c) + sib_in[lax.rem(k, SLOTS), d].astype(jnp.float32)

    def stage_a(k):
        slot = lax.rem(k, SLOTS)
        swap(k).wait_recv()

        @when(k >= SLOTS)
        def _():
            hops_left(k - SLOTS)

        far_out[slot] = mine(k, far).astype(jnp.bfloat16)
        hop_far(k).start()
        dir_out[slot] = mine(k, ways(k)[0]).astype(jnp.bfloat16)
        hop_direct(k).start()

    def stage_b(k):
        slot = lax.rem(k, SLOTS)
        hop_far(k).wait_recv()
        sum_out[slot] = (mine(k, ways(k)[1]) + far_in[slot].astype(jnp.float32)).astype(jnp.bfloat16)
        hop_sum(k).start()

    def stage_c(k):
        slot = lax.rem(k, SLOTS)
        hop_direct(k).wait_recv()
        hop_sum(k).wait_recv()
        total = mine(k, x) + dir_in[slot].astype(jnp.float32) + sum_in[slot].astype(jnp.float32)
        place(k, x)[...] = total.astype(jnp.bfloat16)

    def stage_d(k):
        gather(k, 0, x, ways(k)[0]).start()

    def stage_d1(k):
        gather(k, 1, x, ways(k)[1]).start()

    def stage_e(k):
        forth, back = ways(k)
        gather(k, 0, back, forth).wait_recv()
        gather(k, 2, back, forth).start()
        gather(k, 1, forth, back).wait_recv()

    def stage_f(k):
        forth, back = ways(k)
        gather(k, 2, far, forth).wait_recv()
        pair(k).start()

    def stage_g(k):
        block = out.at[k // chunks_per, pl.ds(0, 3), c, :, columns_of(k)]
        slot = lax.rem(k, AG_SLOTS)
        remote(block, block, ag_send.at[slot], ag_recv.at[0, slot], partner).wait_send()
        pair(k).wait_recv()
        pair(k).wait_send()

    def spread(t):
        return (t // 1) * 1 + lax.rem(t, 1), lax.rem(t, 1) < 1

    def stages(t):
        for stage, (early, late) in ((stage_b, LAG_B), (stage_c, LAG_C)):
            soon, k = t - early < EARLY, t - late
            k = jnp.where(soon, t - early, k)

            @when((k >= 0) & (k < chunks) & (soon | (k >= EARLY)))
            def _():
                stage(k)

        for stage, lag in ((stage_d, 0), (stage_d1, LAG_D1), (stage_e, LAG_E), (stage_f, LAG_F), (stage_g, LAG_G)):
            u = t - lag - LAG_C[0]
            k, there = spread(jnp.maximum(u, 0))

            @when((u >= 0) & there & (k < chunks))
            def _():
                stage(k)

    def tick(t, _):
        busy = t < chunks

        @when(busy)
        def _():
            pass

        stages(t)

        @when(busy)
        def _():
            start_loads(t + 2)
            ready(t)
            part_matmul(t, 0, split)

        @when((t >= 1) & (t <= chunks))
        def _():
            stage_a(t - 1)

        @when(busy)
        def _():
            part_matmul(t, split, rows)
            send_half(t)

        @when(t == chunks + LAG_C[1] + 1)
        def _():
            def drain(i, _):
                k = chunks - SLOTS + i
                swap(k).wait_send()
                hops_left(k)
                return 0

            lax.fori_loop(0, SLOTS, drain, 0)

        return 0

    start_loads(1)
    g_copy(0).wait()
    for i in range(len(cuts) - 1):
        first_copy(i).wait()
        part_matmul(0, cuts[i], cuts[i + 1])
        if i == 0:
            start_loads(2)
    a_copy(1).start()
    pl.semaphore_wait(barrier, 3)
    send_half(0)
    last = ((chunks - 1) // 1) * 1 + (chunks - 1) % 1
    lax.fori_loop(1, LAG_C[0] + last + LAG_G + 1, tick, 0)


def solution(mesh):
    group = mesh.shape["dp"]
    chips = group // CORES

    def local(a, g):
        _, mats, tokens, rows = a.shape
        width = g.shape[-1]
        piece = rows // group
        chunks_per = width // COLS
        chunks = mats * chunks_per
        shape = (mats, chips, CORES, piece, width)
        bf16, f32 = jnp.bfloat16, jnp.float32
        many, one = (SLOTS, chips, piece, COLS), (SLOTS, piece, COLS)
        dma = pltpu.SemaphoreType.DMA
        flops = 2 * mats * tokens * rows * width
        sums = pl.pallas_call(
            functools.partial(kernel, chips, mats, chunks_per, COLS),
            out_shape=pltpu.VMEM(shape, bf16),
            in_specs=[pl.BlockSpec(memory_space=pl.ANY)] * 2,
            out_specs=pl.BlockSpec(memory_space=pltpu.VMEM),
            scratch_shapes=[
                pltpu.VMEM((2, tokens, rows), bf16),
                pltpu.VMEM((G_SLOTS, tokens, COLS), bf16),
                pltpu.VMEM((ACCS, rows, COLS), f32),
                pltpu.VMEM(many, bf16), pltpu.VMEM(many, bf16),
                pltpu.VMEM(one, bf16), pltpu.VMEM(one, bf16),
                pltpu.VMEM(one, bf16), pltpu.VMEM(one, bf16),
                pltpu.VMEM(one, bf16), pltpu.VMEM(one, bf16),
                dma((2,)), dma((1,)), dma((G_SLOTS,)),
                dma((2, SLOTS)), dma((4, SLOTS)),
                dma((AG_SLOTS,)), dma((3, AG_SLOTS)),
                dma((AG_SLOTS,)), dma((AG_SLOTS,)),
            ],
            compiler_params=pltpu.CompilerParams(collective_id=0, has_side_effects=True, vmem_limit_bytes=VMEM_LIMIT),
            cost_estimate=pl.CostEstimate(flops=flops, bytes_accessed=a.nbytes + g.nbytes, transcendentals=0),
            name="grad_sums",
        )(a.reshape(a.shape[1:]), g.reshape(g.shape[1:]))
        return sums.reshape(mats, rows, width)

    return jax.shard_map(local, mesh=mesh, in_specs=(P(("rep", "dp")),) * 2, out_specs=P("rep"), check_vma=False)


VMEM_LIMIT = 44 * 2**20
```

time: 177 us -> 173 us (0.977)
  Pallas kernels: 170 us -> 167 us
    pallas_call x1, Pallas kernels: 170 us -> 167 us  [local(): pl.pallas_call(functools.partial(kernel, chips, mats, chunks_per, COLS),...]
where the time goes in v3:
time: 173 us
  Pallas kernels  167 us (97%)
  local copies, waits for them, and re-layouts  6.68 us (4%)
    pallas_call x1, Pallas kernels, local(): pl.pallas_call(functools.partial(kernel, chips, mats, chunks_per, COLS),...  167 us
    unnamed x1, local copies, waits for them, and re-layouts  6.68 us

profile of v3, /device:TPU:113, one launch (start us, length us, event | category | flops | bytes accessed | tf_op | source)
XLA Modules:
  0.0 173.2 jit_solution(1645722572551404664)
XLA Ops:
  0.0 166.5 %grad_sums.1 = bf16[4,4,2,112,2560]{4,3,2,1,0:T(8,128)(2,1)S(1)} custom-call(bf16[4,4096,896]{2,1,0:T(8,128)(2,1)} %bitcast.4, bf16[4,4096,2560]{2,1,0:T(8,128)(2,1)} %bitcast.1.g_hbm), custom_call_target="tpu_custom_call" | custom-call | flops 75161927680 | bytes 113246208 | tf_op jit(solution)/shard_map/grad_sums/pallas_call | solution.py:283
  166.5 6.7 %copy.4 = bf16[4,896,2560]{2,1,0:T(8,128)(2,1)} copy(bf16[4,896,2560]{2,1,0:T(8,128)(2,1)S(1)} %bitcast.3) | data formatting | bytes 36700160

commit v4 on v3

--- a/solution.py
+++ b/solution.py
@@ -10,17 +10,13 @@
 MESH = pl.DeviceIdType.MESH
 CORES = 2
 COLS = 256
+BLOCKS = 4
 SLOTS = 12
 ACCS = 7
 G_SLOTS = 3
 AG_SLOTS = 12
-EARLY = 0
-LAG_A, LAG_B, LAG_C = (1, 1), (3, 3), (5, 5)
-LAG_D1, LAG_E, LAG_F, LAG_G = 0, 4, 7, 9
-
-
-def when(cond):
-    return pl.when(cond)
+LAG_A, LAG_B, LAG_C = 1, 3, 5
+LAG_E, LAG_F, LAG_G = 4, 8, 10
 
 
 def kernel(chips, mats, chunks_per, cols, a_hbm, g_hbm, out, a_buf, g_buf, acc, sib_out, sib_in, far_out, far_in,
@@ -31,7 +27,7 @@
     tokens = a_hbm.shape[1]
     rows = a_hbm.shape[2]
     piece = rows // (chips * CORES)
-    cuts = [0, rows]
+    step = tokens // BLOCKS
     split = -(-rows // 256) * 128
     partner = {"dp": x * CORES + (1 - c)}
 
@@ -45,14 +41,15 @@
         s = 1 - 2 * lax.rem(k, 2)
         return chip(s), chip(-s)
 
-    far = chip(2)
+    far = chip(chips // 2)
 
     def a_copy(n):
         return pltpu.make_async_copy(a_hbm.at[n], a_buf.at[lax.rem(n, 2)], a_sem.at[lax.rem(n, 2)])
 
-    def first_copy(i):
-        part = pl.ds(cuts[i], cuts[i + 1] - cuts[i])
-        return pltpu.make_async_copy(a_hbm.at[0, :, part], a_buf.at[0, :, part], first_sem.at[i])
+    def first_copies(b):
+        part = pl.ds(pl.multiple_of(b * step, step), step)
+        return (pltpu.make_async_copy(a_hbm.at[0, part], a_buf.at[0, part], first_sem.at[0, b]),
+                pltpu.make_async_copy(g_hbm.at[0, part, pl.ds(0, cols)], g_buf.at[0, part], first_sem.at[1, b]))
 
     def g_copy(k):
         slot = lax.rem(k, G_SLOTS)
@@ -98,15 +95,15 @@
         slot = lax.rem(k, AG_SLOTS)
         return remote(block, block, pair_send.at[slot], pair_recv.at[slot], partner)
 
-    g_copy(0).start()
-    for i in range(len(cuts) - 1):
-        first_copy(i).start()
+    for b in range(BLOCKS):
+        for copy in first_copies(b):
+            copy.start()
     barrier = pltpu.get_barrier_semaphore()
     for to in (partner, at(chip(1)), at(chip(-1))):
         pl.semaphore_signal(barrier, inc=1, device_id=to, device_id_type=MESH)
 
     def send_half(k):
-        @when(k >= SLOTS)
+        @pl.when(k >= SLOTS)
         def _():
             swap(k - SLOTS).wait_send()
 
@@ -122,18 +119,18 @@
                                (((0,), (0,)), ((), ())), preferred_element_type=jnp.float32)
 
     def start_loads(k):
-        @when(k < chunks)
+        @pl.when(k < chunks)
         def _():
             g_copy(k).start()
 
     def ready(k):
         n, first = k // chunks_per, lax.rem(k, chunks_per) == 0
 
-        @when(first & (n + 1 < mats))
+        @pl.when(first & (n + 1 < mats))
         def _():
             a_copy(n + 1).start()
 
-        @when(first)
+        @pl.when(first)
         def _():
             a_copy(n).wait()
 
@@ -149,7 +146,7 @@
         slot = lax.rem(k, SLOTS)
         swap(k).wait_recv()
 
-        @when(k >= SLOTS)
+        @pl.when(k >= SLOTS)
         def _():
             hops_left(k - SLOTS)
 
@@ -173,8 +170,6 @@
 
     def stage_d(k):
         gather(k, 0, x, ways(k)[0]).start()
-
-    def stage_d1(k):
         gather(k, 1, x, ways(k)[1]).start()
 
     def stage_e(k):
@@ -195,51 +190,37 @@
         pair(k).wait_recv()
         pair(k).wait_send()
 
-    def spread(t):
-        return (t // 1) * 1 + lax.rem(t, 1), lax.rem(t, 1) < 1
-
     def stages(t):
-        for stage, (early, late) in ((stage_b, LAG_B), (stage_c, LAG_C)):
-            soon, k = t - early < EARLY, t - late
-            k = jnp.where(soon, t - early, k)
-
-            @when((k >= 0) & (k < chunks) & (soon | (k >= EARLY)))
+        lags = ((stage_b, LAG_B), (stage_c, LAG_C), (stage_d, LAG_C), (stage_e, LAG_C + LAG_E), (stage_f, LAG_C + LAG_F),
+                (stage_g, LAG_C + LAG_G))
+        for stage, lag in lags:
+            k = t - lag
+
+            @pl.when((k >= 0) & (k < chunks))
             def _():
                 stage(k)
 
-        for stage, lag in ((stage_d, 0), (stage_d1, LAG_D1), (stage_e, LAG_E), (stage_f, LAG_F), (stage_g, LAG_G)):
-            u = t - lag - LAG_C[0]
-            k, there = spread(jnp.maximum(u, 0))
-
-            @when((u >= 0) & there & (k < chunks))
-            def _():
-                stage(k)
-
     def tick(t, _):
         busy = t < chunks
 
-        @when(busy)
-        def _():
-            pass
-
         stages(t)
 
-        @when(busy)
+        @pl.when(busy)
         def _():
             start_loads(t + 2)
             ready(t)
             part_matmul(t, 0, split)
 
-        @when((t >= 1) & (t <= chunks))
-        def _():
-            stage_a(t - 1)
-
-        @when(busy)
+        @pl.when(t - LAG_A < chunks)
+        def _():
+            stage_a(t - LAG_A)
+
+        @pl.when(busy)
         def _():
             part_matmul(t, split, rows)
             send_half(t)
 
-        @when(t == chunks + LAG_C[1] + 1)
+        @pl.when(t == chunks + LAG_C + 1)
         def _():
             def drain(i, _):
                 k = chunks - SLOTS + i
@@ -251,18 +232,36 @@
 
         return 0
 
-    start_loads(1)
-    g_copy(0).wait()
-    for i in range(len(cuts) - 1):
-        first_copy(i).wait()
-        part_matmul(0, cuts[i], cuts[i + 1])
-        if i == 0:
-            start_loads(2)
+    acc[0] = jnp.zeros(acc.shape[1:], jnp.float32)
+
+    def first_part(b, _):
+        for copy in first_copies(b):
+            copy.wait()
+
+        @pl.when(b == BLOCKS // 2)
+        def _():
+            start_loads(1)
+
+        acc[0] += multiply(0, pl.ds(pl.multiple_of(b * step, step), step), pl.ds(0, rows))
+        return 0
+
+    lax.fori_loop(0, BLOCKS, first_part, 0)
+    start_loads(2)
     a_copy(1).start()
     pl.semaphore_wait(barrier, 3)
     send_half(0)
-    last = ((chunks - 1) // 1) * 1 + (chunks - 1) % 1
-    lax.fori_loop(1, LAG_C[0] + last + LAG_G + 1, tick, 0)
+    lax.fori_loop(1, chunks + LAG_C + LAG_G, tick, 0)
+
+
+def settle(parts, sums, out, sem):
+    def copy(i):
+        at = i // sums.shape[1], i % sums.shape[1]
+        return pltpu.make_async_copy(sums.at[at], out.at[at], sem.at[i])
+
+    for i in range(parts):
+        copy(i).start()
+    for i in range(parts):
+        copy(i).wait()
 
 
 def solution(mesh):
@@ -293,7 +292,7 @@
                 pltpu.VMEM(one, bf16), pltpu.VMEM(one, bf16),
                 pltpu.VMEM(one, bf16), pltpu.VMEM(one, bf16),
                 pltpu.VMEM(one, bf16), pltpu.VMEM(one, bf16),
-                dma((2,)), dma((1,)), dma((G_SLOTS,)),
+                dma((2,)), dma((2, BLOCKS)), dma((G_SLOTS,)),
                 dma((2, SLOTS)), dma((4, SLOTS)),
                 dma((AG_SLOTS,)), dma((3, AG_SLOTS)),
                 dma((AG_SLOTS,)), dma((AG_SLOTS,)),
@@ -302,7 +301,16 @@
             cost_estimate=pl.CostEstimate(flops=flops, bytes_accessed=a.nbytes + g.nbytes, transcendentals=0),
             name="grad_sums",
         )(a.reshape(a.shape[1:]), g.reshape(g.shape[1:]))
-        return sums.reshape(mats, rows, width)
+        whole = pl.pallas_call(
+            functools.partial(settle, mats * chips),
+            out_shape=jax.ShapeDtypeStruct(shape, bf16),
+            in_specs=[pl.BlockSpec(memory_space=pltpu.VMEM)],
+            out_specs=pl.BlockSpec(memory_space=pl.ANY),
+            scratch_shapes=[dma((mats * chips,))],
+            compiler_params=pltpu.CompilerParams(vmem_limit_bytes=2**20),
+            name="settle",
+        )(pltpu.with_memory_space_constraint(sums, pltpu.VMEM))
+        return whole.reshape(mats, rows, width)
 
     return jax.shard_map(local, mesh=mesh, in_specs=(P(("rep", "dp")),) * 2, out_specs=P("rep"), check_vma=False)
 

time: 173 us -> 172 us (level)
  local copies, waits for them, and re-layouts: 6.68 us -> 0 us
  Pallas kernels: 167 us -> 171 us
    unnamed x1 -> x0, local copies, waits for them, and re-layouts: 6.68 us -> none
    pallas_call x0 -> x1, Pallas kernels: none -> 6.45 us  [local(): pl.pallas_call(functools.partial(settle, mats * chips), out_shape=jax.Sha...]
where the time goes in v4:
time: 172 us; the launch traced here: 171 us
  Pallas kernels  171 us (99%)
    pallas_call x1, Pallas kernels, local(): pl.pallas_call(functools.partial(kernel, chips, mats, chunks_per, COLS),...  165 us
    pallas_call x1, Pallas kernels, local(): pl.pallas_call(functools.partial(settle, mats * chips), out_shape=jax.Sha...  6.45 us

profile of v4, /device:TPU:113, one launch (start us, length us, event | category | flops | bytes accessed | tf_op | source)
XLA Modules:
  0.0 171.5 jit_solution(4995194710184334133)
XLA Ops:
  0.0 165.0 %grad_sums.1.sums = bf16[4,4,2,112,2560]{4,3,2,1,0:T(8,128)(2,1)S(1)} custom-call(bf16[4,4096,896]{2,1,0:T(8,128)(2,1)} %bitcast.3, bf16[4,4096,2560]{2,1,0:T(8,128)(2,1)} %bitcast.1.g_hbm), custom_call_target="tpu_custom_call" | custom-call | flops 75161927680 | bytes 113246208 | tf_op jit(solution)/shard_map/grad_sums/pallas_call | solution.py:282
  165.1 6.4 %settle.1 = bf16[4,4,2,112,2560]{4,3,2,1,0:T(8,128)(2,1)} custom-call(bf16[4,4,2,112,2560]{4,3,2,1,0:T(8,128)(2,1)S(1)} %grad_sums.1.sums), custom_call_target="tpu_custom_call" | custom-call | tf_op jit(solution)/shard_map/settle/pallas_call | solution.py:304
